TPU v7x, 32 devices: a whole 2x2x4 slice. The times are simulated.
32 devices in a mesh: dp: 8 (over z, y), tensor: 4 (over x, core).
Axes of the slice: x: 2, y: 2, z: 4, core: 2. Of those that a mesh axis runs over, the one named last changes fastest.
Arguments:
- inputs: float32 [1024, 16, 512], P('tensor', 'dp'), may hold values from -6 to 6
- qkv_weight: bfloat16 [3, 512, 512], P(None, 'dp', 'tensor'), may hold values from -0.375 to 0.375
- out_weight: bfloat16 [512, 512], P('tensor', 'dp'), may hold values from -1 to 1
- up_weight: bfloat16 [512, 2048], P('dp', 'tensor'), may hold values from -0.25 to 0.25
- down_weight: bfloat16 [2048, 512], P('tensor', 'dp'), may hold values from -0.125 to 0.125
- gain_one: float32 [512], replicated, may hold values from 0.1 to 1.9
- shift_one: float32 [512], replicated, may hold values from -1.5 to 1.5
- gain_two: float32 [512], replicated, may hold values from 0.1 to 1.9
- shift_two: float32 [512], replicated, may hold values from -1.5 to 1.5
- lengths: int32 [16], P('dp'), may hold values from 512 to 1024, as said below
- teacher: float32 [1024, 16, 512], P('tensor', 'dp'), may hold values from -6 to 6
- cotangent: float32 [1024, 16, 512], P('tensor', 'dp'), may hold values from -6 to 6
Outputs:
- output: float32 [1024, 16, 512], P('tensor', 'dp')
- loss: float32 [], replicated
- grad_inputs: float32 [1024, 16, 512], P('tensor', 'dp')
- grad_qkv: float32 [3, 512, 512], P(None, 'dp', 'tensor')
- grad_out_weight: float32 [512, 512], P('tensor', 'dp')
- grad_up: float32 [512, 2048], P('dp', 'tensor')
- grad_down_weight: float32 [2048, 512], P('tensor', 'dp')
- grad_gain_one: float32 [512], replicated
- grad_shift_one: float32 [512], replicated
- grad_gain_two: float32 [512], replicated
- grad_shift_two: float32 [512], replicated
Inputs may be any that keep to these rules, and one draw needn't show every extreme that they name: `lengths`: some sequence has exactly 1024 valid tokens and some has exactly 512.
All inputs are finite; a program needn't handle non-finite values.
Results may differ from a plain program's by a relative error of at most 0.006.
The roundings to bfloat16 on the way count: a program that leaves them out, or rounds other values in their place, can miss the bound.
Values may be sent and summed in bfloat16 or wider, within the bound.
A program may use at most 128 MiB of HBM per device.

v0:
```python
from functools import partial
import math
import jax
import jax.numpy as jnp
from jax import lax
from jax.sharding import PartitionSpec as P

HD = 64


def norm_rows(values, gain, shift):
    center = values - jnp.mean(values, -1, keepdims=True)
    spread = jnp.mean(center * center, -1, keepdims=True)
    return center * lax.rsqrt(spread + 1e-05) * gain + shift


def angle_tables(positions, width):
    half = width // 2
    rates = jnp.exp(jnp.arange(half, dtype=jnp.float32) * (-2.0 * math.log(10000.0) / width))
    angles = positions.astype(jnp.float32)[:, None] * rates[None, :]
    cosine = jnp.concatenate([jnp.cos(angles), jnp.cos(angles)], -1)[:, None, None, :]
    sine = jnp.concatenate([jnp.sin(angles), jnp.sin(angles)], -1)[:, None, None, :]
    return (cosine, sine)


def turn_half(values):
    half = values.shape[-1] // 2
    return jnp.concatenate([-values[..., half:], values[..., :half]], -1)


def rotate(values, cosine, sine):
    return values * cosine + turn_half(values) * sine


def rotate_back(grads, cosine, sine):
    return grads * cosine - turn_half(grads * sine)


def shards(
    inputs,
    qkv_weight,
    out_weight,
    up_weight,
    down_weight,
    gain_one,
    shift_one,
    gain_two,
    shift_two,
    lengths,
    teacher,
    cotangent,
):
    tensor_size = lax.axis_size("tensor")
    own_rows, sequences, width = inputs.shape
    full_rows = own_rows * tensor_size
    local_width = qkv_weight.shape[2]
    local_heads = local_width // HD
    scale = HD ** (-0.5)
    block_rows = min(512, full_rows)
    starts = list(range(0, full_rows, block_rows))
    total = lax.psum(jnp.sum(lengths).astype(jnp.float32), "dp")
    positions = jnp.arange(full_rows)
    cosine, sine = angle_tables(positions, HD)
    own_positions = lax.axis_index("tensor") * own_rows + jnp.arange(own_rows)
    valid = (own_positions[:, None] < lengths[None, :]).astype(jnp.float32)[:, :, None]

    def allowed_for(start_row):
        query_pos = start_row + jnp.arange(block_rows)
        causal = positions[None, None, None, :] <= query_pos[None, None, :, None]
        return causal & (positions[None, None, None, :] < lengths[:, None, None, None])

    qkv_full, out_full = (
        lax.all_gather(qkv_weight, "dp", axis=1, tiled=True),
        lax.all_gather(out_weight, "dp", axis=1, tiled=True),
    )
    normed = norm_rows(inputs, gain_one, shift_one).astype(jnp.bfloat16)
    normed_all = lax.all_gather(normed, "tensor", axis=0, tiled=True)
    projected = jnp.einsum(
        "lsd,cdk->clsk", normed_all, qkv_full, preferred_element_type=jnp.float32
    )
    shaped = projected.reshape(3, full_rows, sequences, local_heads, HD)
    queries = rotate(shaped[0], cosine, sine).astype(jnp.bfloat16)
    keys_all = rotate(shaped[1], cosine, sine).astype(jnp.bfloat16)
    values_all = shaped[2].astype(jnp.bfloat16)

    def block_scores(start_row):
        block_queries = queries[start_row : start_row + block_rows]
        raw = jnp.einsum(
            "qshe,kshe->shqk", block_queries, keys_all, preferred_element_type=jnp.float32
        )
        return jnp.where(allowed_for(start_row), raw * scale, -1e30)

    mixed_blocks = []
    log_sums = []
    for start_row in starts:
        scores = block_scores(start_row)
        highest = jnp.max(scores, -1, keepdims=True)
        expd = jnp.exp(scores - highest)
        denom = jnp.sum(expd, -1, keepdims=True)
        probs = expd / denom
        log_sums.append(highest + jnp.log(denom))
        mixed_blocks.append(
            jnp.einsum(
                "shqk,kshe->qshe",
                probs.astype(jnp.bfloat16),
                values_all,
                preferred_element_type=jnp.float32,
            )
        )
    attended = (
        jnp.concatenate(mixed_blocks, 0)
        .reshape(full_rows, sequences, local_width)
        .astype(jnp.bfloat16)
    )
    slice_part = attended
    middle_state = inputs + lax.psum_scatter(
        jnp.einsum("lsk,kd->lsd", slice_part, out_full, preferred_element_type=jnp.float32),
        "tensor",
        scatter_dimension=0,
        tiled=True,
    )
    up_weight_gathered, down_weight_gathered = (
        lax.all_gather(up_weight, "dp", axis=0, tiled=True),
        lax.all_gather(down_weight, "dp", axis=1, tiled=True),
    )
    second_normed_rows = norm_rows(middle_state, gain_two, shift_two).astype(jnp.bfloat16)
    second_normed_gathered = lax.all_gather(second_normed_rows, "tensor", axis=0, tiled=True)
    activation_input = jnp.einsum(
        "agm,mt->agt",
        second_normed_gathered,
        up_weight_gathered,
        preferred_element_type=jnp.float32,
    )
    hidden_rows = jax.nn.gelu(activation_input, approximate=False).astype(jnp.bfloat16)
    slice_part = hidden_rows
    output = middle_state + lax.psum_scatter(
        jnp.einsum(
            "bzv,vc->bzc", slice_part, down_weight_gathered, preferred_element_type=jnp.float32
        ),
        "tensor",
        scatter_dimension=0,
        tiled=True,
    )
    differ = output - teacher
    square_part = jnp.sum(valid * differ * differ)
    factor = float(full_rows * sequences * lax.axis_size("dp")) / total
    seed = factor * valid * (cotangent + differ)
    unused_value, gelu_back = jax.vjp(partial(jax.nn.gelu, approximate=False), activation_input)
    grad_output_rows = lax.all_gather(seed.astype(jnp.bfloat16), "tensor", axis=0, tiled=True)
    grad_down_weight = jnp.einsum(
        "aoi,aop->ip", hidden_rows, grad_output_rows, preferred_element_type=jnp.float32
    )
    grad_hidden = jnp.einsum(
        "ecb,gb->ecg", grad_output_rows, down_weight_gathered, preferred_element_type=jnp.float32
    )
    grad_activation_input = gelu_back(grad_hidden)[0].astype(jnp.bfloat16)
    grad_up = jnp.einsum(
        "ckr,ckn->rn",
        second_normed_gathered,
        grad_activation_input,
        preferred_element_type=jnp.float32,
    )
    slice_part = grad_activation_input
    grad_normed_two = lax.psum_scatter(
        jnp.einsum(
            "bmq,eq->bme", slice_part, up_weight_gathered, preferred_element_type=jnp.float32
        ),
        "tensor",
        scatter_dimension=0,
        tiled=True,
    )
    unused_norm, norm_back_two = jax.vjp(norm_rows, middle_state, gain_two, shift_two)
    grad_middle_norm, grad_gain_two, grad_shift_two = norm_back_two(grad_normed_two)
    grad_middle = seed + grad_middle_norm
    grad_branch_rows = lax.all_gather(
        grad_middle.astype(jnp.bfloat16), "tensor", axis=0, tiled=True
    )
    grad_out_w = jnp.einsum(
        "lsk,lsd->kd", attended, grad_branch_rows, preferred_element_type=jnp.float32
    )
    grad_attended = jnp.einsum(
        "lsd,kd->lsk", grad_branch_rows, out_full, preferred_element_type=jnp.float32
    )
    grad_attended = grad_attended.astype(jnp.bfloat16).reshape(
        full_rows, sequences, local_heads, HD
    )
    grad_keys = jnp.zeros((full_rows, sequences, local_heads, HD), jnp.float32)
    grad_values = jnp.zeros((full_rows, sequences, local_heads, HD), jnp.float32)
    grad_query_blocks = []
    for block_index, start_row in enumerate(starts):
        scores = block_scores(start_row)
        probs = jnp.exp(scores - log_sums[block_index])
        block_grad = grad_attended[start_row : start_row + block_rows]
        grad_probs = jnp.einsum(
            "qshe,kshe->shqk", block_grad, values_all, preferred_element_type=jnp.float32
        )
        inner = jnp.sum(probs * grad_probs, -1, keepdims=True)
        grad_raw = (probs * (grad_probs - inner) * scale).astype(jnp.bfloat16)
        grad_query_blocks.append(
            jnp.einsum("shqk,kshe->qshe", grad_raw, keys_all, preferred_element_type=jnp.float32)
        )
        grad_keys = grad_keys + jnp.einsum(
            "shqk,qshe->kshe",
            grad_raw,
            queries[start_row : start_row + block_rows],
            preferred_element_type=jnp.float32,
        )
        grad_values = grad_values + jnp.einsum(
            "shqk,qshe->kshe",
            probs.astype(jnp.bfloat16),
            block_grad,
            preferred_element_type=jnp.float32,
        )
    grad_queries = jnp.concatenate(grad_query_blocks, 0)
    grad_projected = jnp.stack(
        [rotate_back(grad_queries, cosine, sine), rotate_back(grad_keys, cosine, sine), grad_values]
    )
    grad_projected = grad_projected.astype(jnp.bfloat16).reshape(
        3, full_rows, sequences, local_width
    )
    grad_qkv = jnp.einsum(
        "lsd,clsk->cdk", normed_all, grad_projected, preferred_element_type=jnp.float32
    )
    slice_part = grad_projected
    grad_normed = lax.psum_scatter(
        jnp.einsum("clsk,cdk->lsd", slice_part, qkv_full, preferred_element_type=jnp.float32),
        "tensor",
        scatter_dimension=0,
        tiled=True,
    )
    unused_first, norm_back_one = jax.vjp(norm_rows, inputs, gain_one, shift_one)
    grad_inputs_norm, grad_gain_one, grad_shift_one = norm_back_one(grad_normed)
    grad_inputs = grad_middle + grad_inputs_norm
    grad_qkv, grad_out_w, grad_up, grad_down_weight = (
        lax.psum_scatter(grad_qkv, "dp", scatter_dimension=1, tiled=True),
        lax.psum_scatter(grad_out_w, "dp", scatter_dimension=1, tiled=True),
        lax.psum_scatter(grad_up, "dp", scatter_dimension=0, tiled=True),
        lax.psum_scatter(grad_down_weight, "dp", scatter_dimension=1, tiled=True),
    )
    square_sum, grad_gain_one, grad_shift_one, grad_gain_two, grad_shift_two = lax.psum(
        (square_part, grad_gain_one, grad_shift_one, grad_gain_two, grad_shift_two),
        ("dp", "tensor"),
    )
    loss = square_sum / (total * width)
    return (
        output,
        loss,
        grad_inputs,
        grad_qkv,
        grad_out_w,
        grad_up,
        grad_down_weight,
        grad_gain_one,
        grad_shift_one,
        grad_gain_two,
        grad_shift_two,
    )


def solution(mesh):
    placed = (
        P("tensor", "dp", None),
        P(None, "dp", "tensor"),
        P("tensor", "dp"),
        P("dp", "tensor"),
        P("tensor", "dp"),
        P(),
        P(),
        P(),
        P(),
        P("dp"),
        P("tensor", "dp", None),
        P("tensor", "dp", None),
    )
    return jax.shard_map(
        shards,
        mesh=mesh,
        in_specs=placed,
        out_specs=(
            P("tensor", "dp", None),
            P(),
            P("tensor", "dp", None),
            P(None, "dp", "tensor"),
            P("tensor", "dp"),
            P("dp", "tensor"),
            P("tensor", "dp"),
            P(),
            P(),
            P(),
            P(),
        ),
        check_vma=False,
    )
```

profile of v0, /device:TPU:0, one launch (start us, length us, event | category | flops | bytes accessed | tf_op | source)
XLA Modules:
  0.0 849.0 jit_solution(6604862089245916614)
XLA Ops:
  7.3 1.6 reduce_sum.156
  8.9 1.6 multiply_reduce_fusion.7
  10.5 2.4 add_convert_fusion.2
  13.0 32.3 %all_gather.26 = bf16[128,512]{0,1:T(8,128)(2,1)S(1)} all-gather(bf16[128,64]{0,1:T(8,128)(2,1)S(1)} %copy-done.47), channel_id=1, replica_groups=mesh['dp'=8,'tensor'=4] {'dp'}, dimensions={1}, use_global_device_ids=true | all-gather | bytes 147456 | tf_op jit(solution)/shard_map/all_gather | solution.py:74
  46.8 31.1 %all_gather.25 = bf16[3,512,128]{2,1,0:T(8,128)(2,1)S(1)} all-gather(bf16[3,64,128]{2,1,0:T(8,128)(2,1)S(1)} %copy-done.35), channel_id=1, replica_groups=mesh['dp'=8,'tensor'=4] {'dp'}, dimensions={1}, use_global_device_ids=true | all-gather | bytes 442368 | tf_op jit(solution)/shard_map/all_gather | solution.py:73
  79.4 3.3 fusion.76
  84.6 1.9 fusion.7
  86.5 1.9 fusion.6
  88.5 4.7 fusion.4
  93.2 3.0 fusion.97
  96.3 3.0 fusion.96
  100.1 2.7 fusion.127
  102.9 45.8 %reduce-scatter.8.cloned.1.call-done = f32[256,2,512]{2,0,1:T(8,128)} async-done(((f32[1024,2,512]{2,0,1:T(8,128)}), f32[256,2,512]{2,0,1:T(8,128)}) %reduce-scatter.8.cloned.1.call-update) | async-done | bytes 1048592 | tf_op jit(solution)/shard_map/reduce_scatter | solution.py:116
  148.7 1.5 fusion.167
  151.7 31.6 %all_gather.28 = bf16[512,512]{1,0:T(8,128)(2,1)S(1)} all-gather(bf16[64,512]{1,0:T(8,128)(2,1)S(1)} %copy-done.34), channel_id=1, replica_groups=mesh['dp'=8,'tensor'=4] {'dp'}, dimensions={0}, use_global_device_ids=true | all-gather | bytes 589824 | tf_op jit(solution)/shard_map/all_gather | solution.py:123
  183.3 31.6 %all_gather.29 = bf16[512,512]{0,1:T(8,128)(2,1)S(1)} all-gather(bf16[512,64]{0,1:T(8,128)(2,1)} %param.16), channel_id=1, replica_groups=mesh['dp'=8,'tensor'=4] {'dp'}, dimensions={1}, use_global_device_ids=true | all-gather | bytes 589824 | tf_op jit(solution)/shard_map/all_gather | solution.py:124
  214.9 4.5 fusion.108
  219.4 10.7 %multiply_convert_fusion.2 = (bf16[1024,2,512]{2,0,1:T(8,128)(2,1)S(1)}, f32[1024,2,512]{2,0,1:T(8,128)}) fusion(f32[1024,2,512]{2,0,1:T(8,128)S(1)} %get-tuple-element.113, u8[1024,512]{1,0:T(8,128)(4,1)S(1)} %get-tuple-element.67, u8[1024,512]{1,0:T(8,128)(4,1)S(1)} %get-tuple-element.66), kind=kLoop, calls=%fused_computation.38 | loop fusion | flops 73400320 | bytes 11534336 | tf_op jit(solution)/shard_map/convert_element_type | solution.py:134
  230.1 1.3 copy-done.9
  231.4 3.3 fusion.111
  236.1 21.9 %psum.43 = f32[]{:T(128)} all-reduce(f32[]{:T(128)S(6)} %convert_element_type.90), channel_id=1, replica_groups=mesh['dp'=8,'tensor'=4] {'dp'}, use_global_device_ids=true, to_apply=%region_13.14 | all-reduce | flops 1 | bytes 8 | tf_op jit(solution)/shard_map/psum | solution.py:61
  259.4 20.1 %reduce-scatter.10.cloned.1.call-done = f32[256,2,512]{2,0,1:T(8,128)} async-done(((f32[1024,2,512]{2,0,1:T(8,128)}), f32[256,2,512]{2,0,1:T(8,128)}) %reduce-scatter.10.cloned.1.call-update) | async-done | bytes 1048592 | tf_op jit(solution)/shard_map/reduce_scatter | solution.py:136
  279.6 3.5 fusion.164
  283.1 22.7 %all-gather.9.cloned.1.call-done = bf16[1024,2,512]{2,0,1:T(8,128)(2,1)} async-done(((bf16[256,2,512]{2,0,1:T(8,128)(2,1)}), bf16[1024,2,512]{2,0,1:T(8,128)(2,1)}) %all-gather.9.cloned.1.call-update) | async-done | bytes 2097168 | tf_op jit(solution)/shard_map/all_gather | solution.py:149
  305.8 6.7 add_convert_fusion
  312.5 1.3 copy-done.8
  313.8 3.2 fusion.113
  317.1 44.7 %reduce-scatter.12.cloned.1.call-done = f32[256,2,512]{2,0,1:T(8,128)} async-done(((f32[1024,2,512]{2,0,1:T(8,128)}), f32[256,2,512]{2,0,1:T(8,128)}) %reduce-scatter.12.cloned.1.call-update) | async-done | bytes 1048592 | tf_op jit(solution)/shard_map/reduce_scatter | solution.py:164
  361.8 2.3 multiply_reduce_fusion.2
  364.8 1.6 fusion.163
  369.6 1.3 log_add_fusion.1
  372.2 19.0 %all-gather.11.cloned.1.call-done = bf16[1024,2,512]{2,0,1:T(8,128)(2,1)} async-done(((bf16[256,2,512]{2,0,1:T(8,128)(2,1)}), bf16[1024,2,512]{2,0,1:T(8,128)(2,1)}) %all-gather.11.cloned.1.call-update) | async-done | bytes 2097168 | tf_op jit(solution)/shard_map/all_gather | solution.py:175
  391.2 2.4 convolution_convert_fusion
  395.1 4.5 fusion.172
  399.6 23.6 %fusion.17 = f32[2,2,64,512]{3,2,1,0:T(8,128)} fusion(bf16[1024,2,2,64]{0,3,2,1:T(8,128)(2,1)S(1)} %copy-done.33, f32[2,2,512,1024]{3,2,1,0:T(8,128)} %fusion.172, f32[2,2,512,1024]{3,2,1,0:T(8,128)} %copy-done.6, f32[2,2,512]{2,1,0:T(2,128)S(1)} %copy-done.49, pred[2,512,1024]{2,1,0:T(8,128)(4,1)} %copy-done.16), kind=kOutput, calls=%fused_computation.23 | convolution fusion | flops 291507200 | bytes 18882560 | tf_op jit(solution)/shard_map/shqk,kshe->qshe/dot_general | solution.py:200
  423.2 19.1 %fusion.14 = f32[2,2,64,1024]{3,2,1,0:T(8,128)} fusion(f32[2,2,512,1024]{3,2,1,0:T(8,128)} %fusion.172, f32[2,2,512,1024]{3,2,1,0:T(8,128)} %copy-done.6, f32[2,2,512]{2,1,0:T(2,128)S(1)} %copy-done.49, pred[2,512,1024]{2,1,0:T(8,128)(4,1)} %copy-done.16, bf16[1024,2,2,64]{0,3,2,1:T(8,128)(2,1)} %copy-done.31), kind=kOutput, calls=%fused_computation.22 | convolution fusion | flops 291507200 | bytes 36978688 | tf_op jit(solution)/shard_map/shqk,qshe->kshe/dot_general | solution.py:202
  442.4 4.5 fusion.173
  446.9 5.0 fusion.56
  452.0 3.5 fusion.91
  455.4 2.0 copy.138
  458.5 18.4 %fusion.24 = f32[2,2,64,512]{3,2,1,0:T(8,128)} fusion(bf16[1024,2,2,64]{0,3,2,1:T(8,128)(2,1)} %copy-done.32, f32[2,2,512,1024]{3,2,1,0:T(8,128)} %fusion.173, f32[2,2,512,1024]{3,2,1,0:T(8,128)} %copy-done.5, f32[2,2,512]{2,1,0:T(2,128)S(1)} %copy-done.48, pred[2,512,1024]{2,1,0:T(8,128)(4,1)} %copy-done.14), kind=kOutput, calls=%fused_computation.26 | convolution fusion | flops 291507200 | bytes 18882560 | tf_op jit(solution)/shard_map/shqk,kshe->qshe/dot_general | solution.py:200
  476.9 20.5 %maximum_multiply_fusion.3 = (f32[1024,2,2,64]{0,3,2,1:T(8,128)}, f32[1024,2,2,64]{0,3,2,1:T(8,128)}, f32[1024,2,2,64]{0,3,2,1:T(8,128)}) fusion(f32[512,2,2,64]{0,3,2,1:T(8,128)} %bitcast.122, f32[512,2,2,64]{0,3,2,1:T(8,128)S(1)} %bitcast.121, f32[1024,64]{0,1:T(8,128)S(1)} %copy-done.25, f32[2,2,64,1024]{3,2,1,0:T(8,128)} %fusion.14, ...), kind=kOutput, calls=%fused_computation.107 | convolution fusion | flops 292555776 | bytes 41435136 | tf_op jit(solution)/shard_map/shqk,qshe->kshe/dot_general | solution.py:202
  499.8 1.5 copy.136
  501.3 2.0 copy.134
  504.6 2.3 fusion.105
  506.9 2.1 copy.137
  509.0 1.5 fusion.104
  511.3 3.0 fusion.88
  515.6 4.6 convolution_bitcast_fusion
  520.3 4.7 convolution_bitcast_fusion.2
  525.3 4.5 convolution_bitcast_fusion.1
  532.0 1.8 copy.145
  533.7 2.2 fusion.98
  536.0 1.7 convolution_bitcast_fusion.3
  537.7 56.4 %all-reduce.4.cloned.1.call-done = f32[3,512,128]{2,0,1:T(4,128)} async-done(((f32[3,512,128]{2,0,1:T(4,128)}), f32[3,512,128]{2,0,1:T(4,128)}) %all-reduce.4.cloned.1.call-update) | async-done | bytes 786448
  595.6 45.1 %reduce-scatter.14.cloned.1.call-done = f32[256,2,512]{2,0,1:T(8,128)} async-done(((f32[1024,2,512]{2,0,1:T(8,128)}), f32[256,2,512]{2,0,1:T(8,128)}) %reduce-scatter.14.cloned.1.call-update) | async-done | bytes 1048592 | tf_op jit(solution)/shard_map/reduce_scatter | solution.py:225
  640.7 1.8 fusion.162
  642.5 1.9 multiply_reduce_fusion.3
  644.4 40.0 %all-reduce.1 = (f32[]{:T(128)}, f32[512]{0:T(512)}, f32[512]{0:T(512)}, f32[512]{0:T(512)}, f32[512]{0:T(512)}) all-reduce(f32[]{:T(128)} %fusion.98, f32[512]{0:T(512)S(1)} %get-tuple-element.68, f32[512]{0:T(512)S(1)} %get-tuple-element.73, f32[512]{0:T(512)S(1)} %copy-done.50, ...), channel_id=1, replica_groups=mesh['dp'=8,'tensor'=4] {'dp','tensor'}, use_global_device_ids=true, to_apply=%region_11.12 | all-reduce | flops 2049 | bytes 16392 | tf_op jit(solution)/shard_map/psum | solution.py:240
  684.4 1.7 add_add_fusion.2
  686.2 1.8 copy.146
  688.6 20.3 %reduce-scatter.18.cloned.1.call-done = f32[64,512]{1,0:T(8,128)} async-done(((f32[512,512]{1,0:T(8,128)}), f32[64,512]{1,0:T(8,128)}) %reduce-scatter.18.cloned.1.call-update) | async-done | bytes 131088 | tf_op jit(solution)/shard_map/reduce_scatter | solution.py:237
  708.9 67.1 %reduce-scatter.20.cloned.1.call-done = f32[512,64]{0,1:T(8,128)} async-done(((f32[512,512]{0,1:T(8,128)}), f32[512,64]{0,1:T(8,128)}) %reduce-scatter.20.cloned.1.call-update) | async-done | bytes 131088 | tf_op jit(solution)/shard_map/reduce_scatter | solution.py:238
  776.0 64.8 %reduce-scatter.16.cloned.1.call-done = f32[128,64]{0,1:T(8,128)} async-done(((f32[128,512]{0,1:T(8,128)}), f32[128,64]{0,1:T(8,128)}) %reduce-scatter.16.cloned.1.call-update) | async-done | bytes 32784 | tf_op jit(solution)/shard_map/reduce_scatter | solution.py:236
  (191 shorter events, 24.7 us)
Async XLA Ops:
  7.2 5.8 copy-start.47
  7.2 39.6 %copy-start.35 = (bf16[3,64,128]{2,1,0:T(8,128)(2,1)S(1)}, bf16[3,64,128]{2,1,0:T(8,128)(2,1)}, u32[]{:S(2)}) copy-start(bf16[3,64,128]{2,1,0:T(8,128)(2,1)} %param.13) | copy-start | bytes 147460
  7.2 70.7 %copy-start.52 = (s32[2]{0:T(128)S(1)}, s32[2]{0:T(128)}, u32[]{:S(2)}) copy-start(s32[2]{0:T(128)} %param.21) | copy-start | bytes 28
  7.2 72.2 %all-gather.5.cloned.1.call-start = ((), (), s32[]{:S(2)}) async-start(), calls=%async_computation.7 | async-start | bytes 2621440 | tf_op jit(solution)/shard_map/all_gather | solution.py:77
  10.5 72.2 %copy-start.43 = (f32[256,2]{0,1:T(2,128)}, f32[256,2]{0,1:T(2,128)S(1)}, u32[]{:S(2)}) copy-start(f32[256,2]{0,1:T(2,128)S(1)} %multiply_reduce_fusion.7) | copy-start | bytes 6148
  10.5 72.2 %copy-start.39 = (f32[256,2]{0,1:T(2,128)}, f32[256,2]{0,1:T(2,128)S(1)}, u32[]{:S(2)}) copy-start(f32[256,2]{0,1:T(2,128)S(1)} %fusion.130) | copy-start | bytes 6148
  12.9 135.8 %reduce-scatter.8.cloned.1.call-start = ((), (), s32[]{:S(2)}) async-start(), calls=%async_computation.8 | async-start | bytes 5242880 | tf_op jit(solution)/shard_map/reduce_scatter | solution.py:116
  77.9 4.8 copy-start.19
  79.3 13.9 %copy-start.14 = (pred[2,512,1024]{2,1,0:T(8,128)(4,1)}, pred[2,512,1024]{2,1,0:T(8,128)(4,1)S(1)}, u32[]{:S(2)}) copy-start(pred[2,512,1024]{2,1,0:T(8,128)(4,1)S(1)} %get-tuple-element.108) | copy-start | bytes 3145732
  79.3 16.9 %copy-start.16 = (pred[2,512,1024]{2,1,0:T(8,128)(4,1)}, pred[2,512,1024]{2,1,0:T(8,128)(4,1)S(1)}, u32[]{:S(2)}) copy-start(pred[2,512,1024]{2,1,0:T(8,128)(4,1)S(1)} %get-tuple-element.107) | copy-start | bytes 3145732
  82.8 13.4 %copy-start.10 = (bf16[1,1024,2,128]{1,3,0,2:T(8,128)(2,1)}, bf16[1,1024,2,128]{1,3,0,2:T(8,128)(2,1)S(1)}, u32[]{:S(2)}) copy-start(bf16[1,1024,2,128]{1,3,0,2:T(8,128)(2,1)S(1)} %slice.107) | copy-start | bytes 1572868
  84.6 2.0 copy-start.31
  84.6 2.0 copy-start.32
  86.5 6.7 copy-start.5
  88.5 7.8 copy-start.6
  88.5 7.8 copy-start.36
  93.2 3.0 copy-start.37
  93.2 3.1 copy-start.38
  100.1 48.6 %copy-start = (f32[256,2,512]{2,1,0:T(2,128)S(1)}, f32[256,2,512]{2,1,0:T(2,128)}, u32[]{:S(2)}) copy-start(f32[256,2,512]{2,1,0:T(2,128)} %param.12) | copy-start | bytes 3145732
  102.8 47.7 %copy-start.46 = (f32[512]{0:T(512)S(1)}, f32[512]{0:T(512)}, u32[]{:S(2)}) copy-start(f32[512]{0:T(512)} %param.19) | copy-start | bytes 6148
  102.8 47.7 %copy-start.57 = (f32[512]{0:T(512)S(1)}, f32[512]{0:T(512)}, u32[]{:S(2)}) copy-start(f32[512]{0:T(512)} %param.20) | copy-start | bytes 6148
  102.8 48.8 %copy-start.34 = (bf16[64,512]{1,0:T(8,128)(2,1)S(1)}, bf16[64,512]{1,0:T(8,128)(2,1)}, u32[]{:S(2)}) copy-start(bf16[64,512]{1,0:T(8,128)(2,1)} %param.15) | copy-start | bytes 196612
  102.8 112.0 %all-gather.7.cloned.1.call-start = ((), (), s32[]{:S(2)}) async-start(), calls=%async_computation.9 | async-start | bytes 2621440 | tf_op jit(solution)/shard_map/all_gather | solution.py:127
  151.6 128.0 %reduce-scatter.10.cloned.1.call-start = ((), (), s32[]{:S(2)}) async-start(), calls=%async_computation.10 | async-start | bytes 5242880 | tf_op jit(solution)/shard_map/reduce_scatter | solution.py:136
  183.3 36.1 %copy-start.21 = (bf16[512,512]{1,0:T(8,128)(2,1)}, bf16[512,512]{1,0:T(8,128)(2,1)S(1)}, u32[]{:S(2)}) copy-start(bf16[512,512]{1,0:T(8,128)(2,1)S(1)} %all_gather.28) | copy-start | bytes 1572868
  214.9 15.2 %copy-start.23 = (bf16[512,512]{0,1:T(8,128)(2,1)}, bf16[512,512]{0,1:T(8,128)(2,1)S(1)}, u32[]{:S(2)}) copy-start(bf16[512,512]{0,1:T(8,128)(2,1)S(1)} %all_gather.29) | copy-start | bytes 1572868
  219.4 10.7 %copy-start.18 = (f32[1024,2,512]{2,0,1:T(8,128)}, f32[1024,2,512]{2,0,1:T(8,128)S(1)}, u32[]{:S(2)}) copy-start(f32[1024,2,512]{2,0,1:T(8,128)S(1)} %get-tuple-element.113) | copy-start | bytes 12582916
  231.4 3.4 copy-start.53
  234.8 71.0 %all-gather.9.cloned.1.call-start = ((), (), s32[]{:S(2)}) async-start(), calls=%async_computation.11 | async-start | bytes 2621440 | tf_op jit(solution)/shard_map/all_gather | solution.py:149
  283.1 78.7 %reduce-scatter.12.cloned.1.call-start = ((), (), s32[]{:S(2)}) async-start(), calls=%async_computation.12 | async-start | bytes 5242880 | tf_op jit(solution)/shard_map/reduce_scatter | solution.py:164
  305.8 8.0 copy-start.22
  312.5 1.3 copy-start.8
  317.1 74.1 %all-gather.11.cloned.1.call-start = ((), (), s32[]{:S(2)}) async-start(), calls=%async_computation.13 | async-start | bytes 2621440 | tf_op jit(solution)/shard_map/all_gather | solution.py:175
  361.8 5.7 copy-start.1
  367.5 27.6 %copy-start.11 = (bf16[1,1024,2,128]{1,3,0,2:T(8,128)(2,1)S(1)}, bf16[1,1024,2,128]{1,3,0,2:T(8,128)(2,1)}, u32[]{:S(2)}) copy-start(bf16[1,1024,2,128]{1,3,0,2:T(8,128)(2,1)} %copy-done.10) | copy-start | bytes 1572868
  368.5 225.6 %all-reduce.4.cloned.1.call-start = ((), (), s32[]{:S(2)}) async-start(), calls=%async_computation.18 | async-start | bytes 2097152
  395.1 4.5 copy-start.33
  395.1 4.5 copy-start.49
  423.2 19.2 %copy-start.28 = (bf16[512,2,128]{0,2,1:T(8,128)(2,1)S(1)}, bf16[512,2,128]{0,2,1:T(8,128)(2,1)}, u32[]{:S(2)}) copy-start(bf16[512,2,128]{0,2,1:T(8,128)(2,1)} %get-tuple-element.100) | copy-start | bytes 786436
  442.4 4.6 copy-start.15
  442.4 4.6 copy-start.48
  442.4 9.5 %slice-start = ((s8[8388608]{0:T(1024)(128)(4,1)}), s8[4194304]{0:T(1024)(128)(4,1)S(1)}, s32[]{:S(2)}) async-start(s8[8388608]{0:T(1024)(128)(4,1)} %bitcast.105), calls=%async_computation.19 | async-start | bytes 8388608
  446.9 5.0 slice-start.1
  446.9 5.0 copy-start.17
  446.9 5.0 copy-start.27
  452.0 5.5 copy-start.29
  458.5 18.4 %copy-start.25 = (f32[1024,64]{0,1:T(8,128)S(1)}, f32[1024,64]{0,1:T(8,128)}, u32[]{:S(2)}) copy-start(f32[1024,64]{0,1:T(8,128)} %pad_maximum_fusion.6) | copy-start | bytes 786436
  511.3 4.3 copy-start.20
  515.6 125.2 %reduce-scatter.14.cloned.1.call-start = ((), (), s32[]{:S(2)}) async-start(), calls=%async_computation.14 | async-start | bytes 5242880 | tf_op jit(solution)/shard_map/reduce_scatter | solution.py:225
  520.3 188.6 %reduce-scatter.18.cloned.1.call-start = ((), (), s32[]{:S(2)}) async-start(), calls=%async_computation.16 | async-start | bytes 1179648 | tf_op jit(solution)/shard_map/reduce_scatter | solution.py:237
  525.0 5.6 copy-start.58
  525.0 6.8 copy-start.54
  525.0 6.8 copy-start.56
  525.0 251.0 %reduce-scatter.20.cloned.1.call-start = ((), (), s32[]{:S(2)}) async-start(), calls=%async_computation.17 | async-start | bytes 1179648 | tf_op jit(solution)/shard_map/reduce_scatter | solution.py:238
  529.8 6.1 copy-start.13
  529.9 110.9 %copy-start.41 = (f32[512]{0:T(512)S(1)}, f32[512]{0:T(512)}, u32[]{:S(2)}) copy-start(f32[512]{0:T(512)} %param.17) | copy-start | bytes 6148
  529.9 310.9 %reduce-scatter.16.cloned.1.call-start = ((), (), s32[]{:S(2)}) async-start(), calls=%async_computation.15 | async-start | bytes 294912 | tf_op jit(solution)/shard_map/reduce_scatter | solution.py:236
  531.9 4.1 copy-start.7
  533.7 108.7 %copy-start.44 = (f32[256,2]{0,1:T(2,128)S(1)}, f32[256,2]{0,1:T(2,128)}, u32[]{:S(2)}) copy-start(f32[256,2]{0,1:T(2,128)} %copy-done.43) | copy-start | bytes 6148
  533.7 108.8 %copy-start.40 = (f32[256,2]{0,1:T(2,128)S(1)}, f32[256,2]{0,1:T(2,128)}, u32[]{:S(2)}) copy-start(f32[256,2]{0,1:T(2,128)} %copy-done.39) | copy-start | bytes 6148
  536.0 108.4 %copy-start.50 = (f32[512]{0:T(512)S(1)}, f32[512]{0:T(512)}, u32[]{:S(2)}) copy-start(f32[512]{0:T(512)} %get-tuple-element.70) | copy-start | bytes 6148
  536.0 108.4 %copy-start.51 = (f32[512]{0:T(512)S(1)}, f32[512]{0:T(512)}, u32[]{:S(2)}) copy-start(f32[512]{0:T(512)} %get-tuple-element.72) | copy-start | bytes 6148
  536.0 148.5 %copy-start.2 = (f32[256,2,512]{2,0,1:T(8,128)S(1)}, f32[256,2,512]{2,0,1:T(8,128)}, u32[]{:S(2)}) copy-start(f32[256,2,512]{2,0,1:T(8,128)} %get-tuple-element.83) | copy-start | bytes 3145732
  640.7 43.7 %copy-start.3 = (f32[256,2,512]{2,0,1:T(8,128)S(1)}, f32[256,2,512]{2,0,1:T(8,128)}, u32[]{:S(2)}) copy-start(f32[256,2,512]{2,0,1:T(8,128)} %reduce-scatter.14.cloned.1.call-done) | copy-start | bytes 3145732
  (9 other events, 8.7 us)
Sparse Core Ops, SparseCore 0:
  13.0 25.2 all-gather.4
  103.0 45.6 reduce-scatter.7
  151.7 22.5 all-gather.6
  234.9 44.6 reduce-scatter.9
  283.2 22.5 all-gather.8
  317.2 44.5 reduce-scatter.11
  368.6 22.5 all-gather.10
  515.7 78.2 all-reduce.3
  596.5 44.1 reduce-scatter.13
  644.6 64.2 reduce-scatter.17
  712.9 63.1 reduce-scatter.19
  779.8 60.9 reduce-scatter.15
where the time goes:
time: 853 us; the launch traced here: 849 us
  waiting for transfers between devices  406 us (48%)
  blocking collectives  189 us (22%)
  matrix products  154 us (18%)
  other arithmetic  55.5 us (7%)
  local copies, waits for them, and re-layouts  24.8 us (3%)
  between operations  19.7 us (2%)
    reduce_scatter x1, waiting for transfers between devices, shards(): lax.psum_scatter(grad_down_weight, 'dp', scatter_dimension=1, tiled=True)  67.1 us
    reduce_scatter x1, waiting for transfers between devices, shards(): lax.psum_scatter(grad_out_w, 'dp', scatter_dimension=1, tiled=True)  64.8 us
    unnamed x13, waiting for transfers between devices  56.6 us
    reduce_scatter x1, waiting for transfers between devices, shards(): lax.psum_scatter(jnp.einsum('lsk,kd->lsd', slice_part, out_full, preferre...  45.8 us
    reduce_scatter x1, waiting for transfers between devices, shards(): lax.psum_scatter(jnp.einsum('clsk,cdk->lsd', slice_part, qkv_full, prefer...  45.1 us
    reduce_scatter x1, waiting for transfers between devices, shards(): lax.psum_scatter(jnp.einsum('bmq,eq->bme', slice_part, up_weight_gathered...  44.7 us
    dot_general x2, matrix products, shards(): jnp.einsum('shqk,kshe->qshe', grad_raw, keys_all, preferred_element_type=...  42.1 us
    psum x1, blocking collectives, shards(): lax.psum((square_part, grad_gain_one, grad_shift_one, grad_gain_two, grad...  40 us
  transfers between devices with their start and end apart: 12, of which 10 were waited for; matrix products, arithmetic and copies ran while one was open for 4% of the time, Pallas kernels for 0%

commit v1 on v0

--- a/solution.py
+++ b/solution.py
@@ -58,7 +58,8 @@
     scale = HD ** (-0.5)
     block_rows = min(512, full_rows)
     starts = list(range(0, full_rows, block_rows))
-    total = lax.psum(jnp.sum(lengths).astype(jnp.float32), "dp")
+    point = jnp.sum(lengths).astype(jnp.float32)
+    total = jnp.sum(lax.all_gather(point, "dp"), axis=0)
     positions = jnp.arange(full_rows)
     cosine, sine = angle_tables(positions, HD)
     own_positions = lax.axis_index("tensor") * own_rows + jnp.arange(own_rows)

time: 853 us -> 852 us (level)
    psum x1 -> x0, blocking collectives: 21.9 us -> none  [shards(): total = lax.psum(jnp.sum(lengths).astype(jnp.float32), 'dp')]
    unnamed x0 -> x1, blocking collectives: none -> 21.3 us
where the time goes in v1:
time: 852 us; the launch traced here: 849 us
  waiting for transfers between devices  405 us (48%)
  blocking collectives  188 us (22%)
  matrix products  153 us (18%)
  other arithmetic  56.1 us (7%)
  local copies, waits for them, and re-layouts  25.5 us (3%)
  between operations  19.7 us (2%)
    reduce_scatter x1, waiting for transfers between devices, shards(): lax.psum_scatter(grad_down_weight, 'dp', scatter_dimension=1, tiled=True)  67.1 us
    reduce_scatter x1, waiting for transfers between devices, shards(): lax.psum_scatter(grad_out_w, 'dp', scatter_dimension=1, tiled=True)  64.8 us
    unnamed x13, waiting for transfers between devices  57.1 us
    reduce_scatter x1, waiting for transfers between devices, shards(): lax.psum_scatter(jnp.einsum('lsk,kd->lsd', slice_part, out_full, preferre...  45.8 us
    reduce_scatter x1, waiting for transfers between devices, shards(): lax.psum_scatter(jnp.einsum('clsk,cdk->lsd', slice_part, qkv_full, prefer...  45.1 us
    reduce_scatter x1, waiting for transfers between devices, shards(): lax.psum_scatter(jnp.einsum('bmq,eq->bme', slice_part, up_weight_gathered...  44.7 us
    dot_general x2, matrix products, shards(): jnp.einsum('shqk,kshe->qshe', grad_raw, keys_all, preferred_element_type=...  41.7 us
    psum x1, blocking collectives, shards(): lax.psum((square_part, grad_gain_one, grad_shift_one, grad_gain_two, grad...  40 us
  transfers between devices with their start and end apart: 12, of which 10 were waited for; matrix products, arithmetic and copies ran while one was open for 4% of the time, Pallas kernels for 0%

profile of v1, /device:TPU:0, one launch (start us, length us, event | category | flops | bytes accessed | tf_op | source)
XLA Modules:
  0.0 848.6 jit_solution(13265177248675624915)
XLA Ops:
  7.3 1.6 reduce_sum.167
  8.9 1.6 multiply_reduce_fusion.7
  10.5 2.4 add_convert_fusion.2
  13.0 32.3 %all_gather.32 = bf16[128,512]{0,1:T(8,128)(2,1)S(1)} all-gather(bf16[128,64]{0,1:T(8,128)(2,1)S(1)} %copy-done.47), channel_id=1, replica_groups=mesh['dp'=8,'tensor'=4] {'dp'}, dimensions={1}, use_global_device_ids=true | all-gather | bytes 147456 | tf_op jit(solution)/shard_map/all_gather | solution.py:75
  46.8 31.1 %all_gather.31 = bf16[3,512,128]{2,1,0:T(8,128)(2,1)S(1)} all-gather(bf16[3,64,128]{2,1,0:T(8,128)(2,1)S(1)} %copy-done.35), channel_id=1, replica_groups=mesh['dp'=8,'tensor'=4] {'dp'}, dimensions={1}, use_global_device_ids=true | all-gather | bytes 442368 | tf_op jit(solution)/shard_map/all_gather | solution.py:74
  79.4 3.3 fusion.76
  84.6 1.9 fusion.7
  86.5 1.9 fusion.6
  88.5 4.7 fusion.4
  93.2 3.0 fusion.97
  96.3 3.0 fusion.96
  100.1 2.7 fusion.127
  102.9 45.8 %reduce-scatter.8.cloned.1.call-done = f32[256,2,512]{2,0,1:T(8,128)} async-done(((f32[1024,2,512]{2,0,1:T(8,128)}), f32[256,2,512]{2,0,1:T(8,128)}) %reduce-scatter.8.cloned.1.call-update) | async-done | bytes 1048592 | tf_op jit(solution)/shard_map/reduce_scatter | solution.py:117
  148.7 1.5 fusion.167
  151.6 31.7 %all_gather.34 = bf16[512,512]{1,0:T(8,128)(2,1)S(1)} all-gather(bf16[64,512]{1,0:T(8,128)(2,1)S(1)} %copy-done.34), channel_id=1, replica_groups=mesh['dp'=8,'tensor'=4] {'dp'}, dimensions={0}, use_global_device_ids=true | all-gather | bytes 589824 | tf_op jit(solution)/shard_map/all_gather | solution.py:124
  183.3 31.6 %all_gather.35 = bf16[512,512]{0,1:T(8,128)(2,1)S(1)} all-gather(bf16[512,64]{0,1:T(8,128)(2,1)} %param.16), channel_id=1, replica_groups=mesh['dp'=8,'tensor'=4] {'dp'}, dimensions={1}, use_global_device_ids=true | all-gather | bytes 589824 | tf_op jit(solution)/shard_map/all_gather | solution.py:125
  214.9 4.5 fusion.108
  219.4 10.7 %multiply_convert_fusion.2 = (bf16[1024,2,512]{2,0,1:T(8,128)(2,1)S(1)}, f32[1024,2,512]{2,0,1:T(8,128)}) fusion(f32[1024,2,512]{2,0,1:T(8,128)S(1)} %get-tuple-element.115, u8[1024,512]{1,0:T(8,128)(4,1)S(1)} %get-tuple-element.67, u8[1024,512]{1,0:T(8,128)(4,1)S(1)} %get-tuple-element.66), kind=kLoop, calls=%fused_computation.38 | loop fusion | flops 73400320 | bytes 11534336 | tf_op jit(solution)/shard_map/convert_element_type | solution.py:135
  231.5 3.3 fusion.111
  237.5 21.3 %all-reduce = f32[8]{0:T(128)S(1)} all-reduce(f32[8]{0:T(128)S(1)} %dynamic-update-slice), channel_id=1, replica_groups=mesh['dp'=8,'tensor'=4] {'dp'}, use_global_device_ids=true, to_apply=%add | all-reduce | flops 8 | bytes 64
  260.8 18.7 %reduce-scatter.10.cloned.1.call-done = f32[256,2,512]{2,0,1:T(8,128)} async-done(((f32[1024,2,512]{2,0,1:T(8,128)}), f32[256,2,512]{2,0,1:T(8,128)}) %reduce-scatter.10.cloned.1.call-update) | async-done | bytes 1048592 | tf_op jit(solution)/shard_map/reduce_scatter | solution.py:137
  279.5 3.5 fusion.164
  283.1 22.7 %all-gather.9.cloned.1.call-done = bf16[1024,2,512]{2,0,1:T(8,128)(2,1)} async-done(((bf16[256,2,512]{2,0,1:T(8,128)(2,1)}), bf16[1024,2,512]{2,0,1:T(8,128)(2,1)}) %all-gather.9.cloned.1.call-update) | async-done | bytes 2097168 | tf_op jit(solution)/shard_map/all_gather | solution.py:150
  305.8 6.7 add_convert_fusion
  312.5 1.3 copy-done.7
  313.8 3.2 fusion.113
  317.1 44.7 %reduce-scatter.12.cloned.1.call-done = f32[256,2,512]{2,0,1:T(8,128)} async-done(((f32[1024,2,512]{2,0,1:T(8,128)}), f32[256,2,512]{2,0,1:T(8,128)}) %reduce-scatter.12.cloned.1.call-update) | async-done | bytes 1048592 | tf_op jit(solution)/shard_map/reduce_scatter | solution.py:165
  361.8 2.3 multiply_reduce_fusion.2
  364.8 1.6 fusion.163
  369.9 1.3 log_add_fusion.1
  371.3 1.3 log_add_fusion
  372.6 18.6 %all-gather.11.cloned.1.call-done = bf16[1024,2,512]{2,0,1:T(8,128)(2,1)} async-done(((bf16[256,2,512]{2,0,1:T(8,128)(2,1)}), bf16[1024,2,512]{2,0,1:T(8,128)(2,1)}) %all-gather.11.cloned.1.call-update) | async-done | bytes 2097168 | tf_op jit(solution)/shard_map/all_gather | solution.py:176
  391.2 2.4 convolution_convert_fusion
  395.0 4.5 fusion.173
  399.6 23.3 %fusion.17 = f32[2,2,64,512]{3,2,1,0:T(8,128)} fusion(bf16[1024,2,2,64]{0,3,2,1:T(8,128)(2,1)S(1)} %copy-done.33, f32[2,2,512,1024]{3,2,1,0:T(8,128)} %fusion.173, f32[2,2,512,1024]{3,2,1,0:T(8,128)} %copy-done.6, f32[2,2,512]{2,1,0:T(2,128)S(1)} %copy-done.49, pred[2,512,1024]{2,1,0:T(8,128)(4,1)} %copy-done.16), kind=kOutput, calls=%fused_computation.23 | convolution fusion | flops 291507200 | bytes 18882560 | tf_op jit(solution)/shard_map/shqk,kshe->qshe/dot_general | solution.py:201
  422.8 19.2 %fusion.14 = f32[2,2,64,1024]{3,2,1,0:T(8,128)} fusion(f32[2,2,512,1024]{3,2,1,0:T(8,128)} %fusion.173, f32[2,2,512,1024]{3,2,1,0:T(8,128)} %copy-done.6, f32[2,2,512]{2,1,0:T(2,128)S(1)} %copy-done.49, pred[2,512,1024]{2,1,0:T(8,128)(4,1)} %copy-done.16, bf16[1024,2,2,64]{0,3,2,1:T(8,128)(2,1)} %copy-done.31), kind=kOutput, calls=%fused_computation.22 | convolution fusion | flops 291507200 | bytes 36978688 | tf_op jit(solution)/shard_map/shqk,qshe->kshe/dot_general | solution.py:203
  442.0 4.5 fusion.174
  446.6 5.0 fusion.56
  451.6 3.5 fusion.91
  455.0 2.1 copy.138
  458.1 18.4 %fusion.24 = f32[2,2,64,512]{3,2,1,0:T(8,128)} fusion(bf16[1024,2,2,64]{0,3,2,1:T(8,128)(2,1)} %copy-done.32, f32[2,2,512,1024]{3,2,1,0:T(8,128)} %fusion.174, f32[2,2,512,1024]{3,2,1,0:T(8,128)} %copy-done.5, f32[2,2,512]{2,1,0:T(2,128)S(1)} %copy-done.48, pred[2,512,1024]{2,1,0:T(8,128)(4,1)} %copy-done.14), kind=kOutput, calls=%fused_computation.26 | convolution fusion | flops 291507200 | bytes 18882560 | tf_op jit(solution)/shard_map/shqk,kshe->qshe/dot_general | solution.py:201
  476.6 20.5 %maximum_multiply_fusion.3 = (f32[1024,2,2,64]{0,3,2,1:T(8,128)}, f32[1024,2,2,64]{0,3,2,1:T(8,128)}, f32[1024,2,2,64]{0,3,2,1:T(8,128)}) fusion(f32[512,2,2,64]{0,3,2,1:T(8,128)} %bitcast.124, f32[512,2,2,64]{0,3,2,1:T(8,128)S(1)} %bitcast.123, f32[1024,64]{0,1:T(8,128)S(1)} %copy-done.25, f32[2,2,64,1024]{3,2,1,0:T(8,128)} %fusion.14, ...), kind=kOutput, calls=%fused_computation.107 | convolution fusion | flops 292555776 | bytes 41435136 | tf_op jit(solution)/shard_map/shqk,qshe->kshe/dot_general | solution.py:203
  499.4 1.5 copy.136
  501.0 2.1 copy.134
  504.3 2.3 fusion.105
  506.6 2.1 copy.137
  508.7 1.5 fusion.104
  511.0 3.0 fusion.88
  515.3 4.6 convolution_bitcast_fusion
  520.0 4.7 convolution_bitcast_fusion.2
  525.0 4.5 convolution_bitcast_fusion.1
  531.0 1.8 copy.145
  532.8 2.2 fusion.98
  535.0 1.7 convolution_bitcast_fusion.3
  536.7 56.9 %all-reduce.5.cloned.1.call-done = f32[3,512,128]{2,0,1:T(4,128)} async-done(((f32[3,512,128]{2,0,1:T(4,128)}), f32[3,512,128]{2,0,1:T(4,128)}) %all-reduce.5.cloned.1.call-update) | async-done | bytes 786448
  595.2 45.1 %reduce-scatter.14.cloned.1.call-done = f32[256,2,512]{2,0,1:T(8,128)} async-done(((f32[1024,2,512]{2,0,1:T(8,128)}), f32[256,2,512]{2,0,1:T(8,128)}) %reduce-scatter.14.cloned.1.call-update) | async-done | bytes 1048592 | tf_op jit(solution)/shard_map/reduce_scatter | solution.py:226
  640.4 1.8 fusion.162
  642.2 1.9 multiply_reduce_fusion.3
  644.0 40.0 %all-reduce.2 = (f32[]{:T(128)}, f32[512]{0:T(512)}, f32[512]{0:T(512)}, f32[512]{0:T(512)}, f32[512]{0:T(512)}) all-reduce(f32[]{:T(128)} %fusion.98, f32[512]{0:T(512)S(1)} %get-tuple-element.68, f32[512]{0:T(512)S(1)} %get-tuple-element.73, f32[512]{0:T(512)S(1)} %copy-done.50, ...), channel_id=1, replica_groups=mesh['dp'=8,'tensor'=4] {'dp','tensor'}, use_global_device_ids=true, to_apply=%region_11.12 | all-reduce | flops 2049 | bytes 16392 | tf_op jit(solution)/shard_map/psum | solution.py:241
  684.1 1.7 add_add_fusion.2
  685.8 1.8 copy.146
  688.3 20.3 %reduce-scatter.18.cloned.1.call-done = f32[64,512]{1,0:T(8,128)} async-done(((f32[512,512]{1,0:T(8,128)}), f32[64,512]{1,0:T(8,128)}) %reduce-scatter.18.cloned.1.call-update) | async-done | bytes 131088 | tf_op jit(solution)/shard_map/reduce_scatter | solution.py:238
  708.5 67.1 %reduce-scatter.20.cloned.1.call-done = f32[512,64]{0,1:T(8,128)} async-done(((f32[512,512]{0,1:T(8,128)}), f32[512,64]{0,1:T(8,128)}) %reduce-scatter.20.cloned.1.call-update) | async-done | bytes 131088 | tf_op jit(solution)/shard_map/reduce_scatter | solution.py:239
  775.7 64.8 %reduce-scatter.16.cloned.1.call-done = f32[128,64]{0,1:T(8,128)} async-done(((f32[128,512]{0,1:T(8,128)}), f32[128,64]{0,1:T(8,128)}) %reduce-scatter.16.cloned.1.call-update) | async-done | bytes 32784 | tf_op jit(solution)/shard_map/reduce_scatter | solution.py:237
  (194 shorter events, 26.4 us)
Async XLA Ops:
  7.2 5.8 copy-start.47
  7.2 39.6 %copy-start.35 = (bf16[3,64,128]{2,1,0:T(8,128)(2,1)S(1)}, bf16[3,64,128]{2,1,0:T(8,128)(2,1)}, u32[]{:S(2)}) copy-start(bf16[3,64,128]{2,1,0:T(8,128)(2,1)} %param.13) | copy-start | bytes 147460
  7.2 70.7 %copy-start.52 = (s32[2]{0:T(128)S(1)}, s32[2]{0:T(128)}, u32[]{:S(2)}) copy-start(s32[2]{0:T(128)} %param.21) | copy-start | bytes 28
  7.2 72.2 %all-gather.5.cloned.1.call-start = ((), (), s32[]{:S(2)}) async-start(), calls=%async_computation.7 | async-start | bytes 2621440 | tf_op jit(solution)/shard_map/all_gather | solution.py:78
  10.5 72.2 %copy-start.43 = (f32[256,2]{0,1:T(2,128)}, f32[256,2]{0,1:T(2,128)S(1)}, u32[]{:S(2)}) copy-start(f32[256,2]{0,1:T(2,128)S(1)} %multiply_reduce_fusion.7) | copy-start | bytes 6148
  10.5 72.2 %copy-start.39 = (f32[256,2]{0,1:T(2,128)}, f32[256,2]{0,1:T(2,128)S(1)}, u32[]{:S(2)}) copy-start(f32[256,2]{0,1:T(2,128)S(1)} %fusion.130) | copy-start | bytes 6148
  12.9 135.7 %reduce-scatter.8.cloned.1.call-start = ((), (), s32[]{:S(2)}) async-start(), calls=%async_computation.8 | async-start | bytes 5242880 | tf_op jit(solution)/shard_map/reduce_scatter | solution.py:117
  77.9 4.8 copy-start.19
  79.3 13.9 %copy-start.14 = (pred[2,512,1024]{2,1,0:T(8,128)(4,1)}, pred[2,512,1024]{2,1,0:T(8,128)(4,1)S(1)}, u32[]{:S(2)}) copy-start(pred[2,512,1024]{2,1,0:T(8,128)(4,1)S(1)} %get-tuple-element.108) | copy-start | bytes 3145732
  79.3 16.9 %copy-start.16 = (pred[2,512,1024]{2,1,0:T(8,128)(4,1)}, pred[2,512,1024]{2,1,0:T(8,128)(4,1)S(1)}, u32[]{:S(2)}) copy-start(pred[2,512,1024]{2,1,0:T(8,128)(4,1)S(1)} %get-tuple-element.107) | copy-start | bytes 3145732
  82.8 13.4 %copy-start.10 = (bf16[1,1024,2,128]{1,3,0,2:T(8,128)(2,1)}, bf16[1,1024,2,128]{1,3,0,2:T(8,128)(2,1)S(1)}, u32[]{:S(2)}) copy-start(bf16[1,1024,2,128]{1,3,0,2:T(8,128)(2,1)S(1)} %slice.107) | copy-start | bytes 1572868
  84.6 2.0 copy-start.31
  84.6 2.0 copy-start.32
  86.5 6.7 copy-start.5
  88.5 7.8 copy-start.6
  88.5 7.8 copy-start.36
  93.2 3.0 copy-start.37
  93.2 3.1 copy-start.38
  100.1 48.5 %copy-start = (f32[256,2,512]{2,1,0:T(2,128)S(1)}, f32[256,2,512]{2,1,0:T(2,128)}, u32[]{:S(2)}) copy-start(f32[256,2,512]{2,1,0:T(2,128)} %param.12) | copy-start | bytes 3145732
  102.8 47.7 %copy-start.46 = (f32[512]{0:T(512)S(1)}, f32[512]{0:T(512)}, u32[]{:S(2)}) copy-start(f32[512]{0:T(512)} %param.19) | copy-start | bytes 6148
  102.8 47.7 %copy-start.57 = (f32[512]{0:T(512)S(1)}, f32[512]{0:T(512)}, u32[]{:S(2)}) copy-start(f32[512]{0:T(512)} %param.20) | copy-start | bytes 6148
  102.8 48.8 %copy-start.34 = (bf16[64,512]{1,0:T(8,128)(2,1)S(1)}, bf16[64,512]{1,0:T(8,128)(2,1)}, u32[]{:S(2)}) copy-start(bf16[64,512]{1,0:T(8,128)(2,1)} %param.15) | copy-start | bytes 196612
  102.9 112.1 %all-gather.7.cloned.1.call-start = ((), (), s32[]{:S(2)}) async-start(), calls=%async_computation.9 | async-start | bytes 2621440 | tf_op jit(solution)/shard_map/all_gather | solution.py:128
  151.6 128.0 %reduce-scatter.10.cloned.1.call-start = ((), (), s32[]{:S(2)}) async-start(), calls=%async_computation.10 | async-start | bytes 5242880 | tf_op jit(solution)/shard_map/reduce_scatter | solution.py:137
  183.3 36.1 %copy-start.21 = (bf16[512,512]{1,0:T(8,128)(2,1)}, bf16[512,512]{1,0:T(8,128)(2,1)S(1)}, u32[]{:S(2)}) copy-start(bf16[512,512]{1,0:T(8,128)(2,1)S(1)} %all_gather.34) | copy-start | bytes 1572868
  214.9 15.2 %copy-start.23 = (bf16[512,512]{0,1:T(8,128)(2,1)}, bf16[512,512]{0,1:T(8,128)(2,1)S(1)}, u32[]{:S(2)}) copy-start(bf16[512,512]{0,1:T(8,128)(2,1)S(1)} %all_gather.35) | copy-start | bytes 1572868
  219.4 10.7 %copy-start.18 = (f32[1024,2,512]{2,0,1:T(8,128)}, f32[1024,2,512]{2,0,1:T(8,128)S(1)}, u32[]{:S(2)}) copy-start(f32[1024,2,512]{2,0,1:T(8,128)S(1)} %get-tuple-element.115) | copy-start | bytes 12582916
  231.5 3.4 copy-start.53
  231.5 4.7 copy-start.58
  234.8 71.0 %all-gather.9.cloned.1.call-start = ((), (), s32[]{:S(2)}) async-start(), calls=%async_computation.11 | async-start | bytes 2621440 | tf_op jit(solution)/shard_map/all_gather | solution.py:150
  283.0 78.7 %reduce-scatter.12.cloned.1.call-start = ((), (), s32[]{:S(2)}) async-start(), calls=%async_computation.12 | async-start | bytes 5242880 | tf_op jit(solution)/shard_map/reduce_scatter | solution.py:165
  305.8 8.0 copy-start.22
  312.4 1.3 copy-start.7
  317.0 74.1 %all-gather.11.cloned.1.call-start = ((), (), s32[]{:S(2)}) async-start(), calls=%async_computation.13 | async-start | bytes 2621440 | tf_op jit(solution)/shard_map/all_gather | solution.py:176
  361.8 5.7 copy-start.1
  367.5 27.6 %copy-start.11 = (bf16[1,1024,2,128]{1,3,0,2:T(8,128)(2,1)S(1)}, bf16[1,1024,2,128]{1,3,0,2:T(8,128)(2,1)}, u32[]{:S(2)}) copy-start(bf16[1,1024,2,128]{1,3,0,2:T(8,128)(2,1)} %copy-done.10) | copy-start | bytes 1572868
  368.4 225.2 %all-reduce.5.cloned.1.call-start = ((), (), s32[]{:S(2)}) async-start(), calls=%async_computation.18 | async-start | bytes 2097152
  395.0 4.5 copy-start.33
  395.0 4.5 copy-start.49
  422.8 19.2 %copy-start.28 = (bf16[512,2,128]{0,2,1:T(8,128)(2,1)S(1)}, bf16[512,2,128]{0,2,1:T(8,128)(2,1)}, u32[]{:S(2)}) copy-start(bf16[512,2,128]{0,2,1:T(8,128)(2,1)} %get-tuple-element.100) | copy-start | bytes 786436
  442.0 4.5 copy-start.15
  442.0 4.5 copy-start.48
  442.0 9.5 %slice-start = ((s8[8388608]{0:T(1024)(128)(4,1)}), s8[4194304]{0:T(1024)(128)(4,1)S(1)}, s32[]{:S(2)}) async-start(s8[8388608]{0:T(1024)(128)(4,1)} %bitcast.107), calls=%async_computation.19 | async-start | bytes 8388608
  446.5 5.0 slice-start.1
  446.5 5.0 copy-start.17
  446.5 5.0 copy-start.27
  451.6 5.5 copy-start.29
  458.1 18.4 %copy-start.25 = (f32[1024,64]{0,1:T(8,128)S(1)}, f32[1024,64]{0,1:T(8,128)}, u32[]{:S(2)}) copy-start(f32[1024,64]{0,1:T(8,128)} %pad_maximum_fusion.6) | copy-start | bytes 786436
  511.0 4.3 copy-start.20
  515.2 125.1 %reduce-scatter.14.cloned.1.call-start = ((), (), s32[]{:S(2)}) async-start(), calls=%async_computation.14 | async-start | bytes 5242880 | tf_op jit(solution)/shard_map/reduce_scatter | solution.py:226
  519.9 188.6 %reduce-scatter.18.cloned.1.call-start = ((), (), s32[]{:S(2)}) async-start(), calls=%async_computation.16 | async-start | bytes 1179648 | tf_op jit(solution)/shard_map/reduce_scatter | solution.py:238
  524.7 6.2 copy-start.54
  524.7 6.2 copy-start.56
  524.7 250.9 %reduce-scatter.20.cloned.1.call-start = ((), (), s32[]{:S(2)}) async-start(), calls=%async_computation.17 | async-start | bytes 1179648 | tf_op jit(solution)/shard_map/reduce_scatter | solution.py:239
  529.5 5.5 copy-start.13
  529.5 110.9 %copy-start.41 = (f32[512]{0:T(512)S(1)}, f32[512]{0:T(512)}, u32[]{:S(2)}) copy-start(f32[512]{0:T(512)} %param.17) | copy-start | bytes 6148
  529.5 310.9 %reduce-scatter.16.cloned.1.call-start = ((), (), s32[]{:S(2)}) async-start(), calls=%async_computation.15 | async-start | bytes 294912 | tf_op jit(solution)/shard_map/reduce_scatter | solution.py:237
  530.9 4.1 copy-start.8
  532.8 109.3 %copy-start.44 = (f32[256,2]{0,1:T(2,128)S(1)}, f32[256,2]{0,1:T(2,128)}, u32[]{:S(2)}) copy-start(f32[256,2]{0,1:T(2,128)} %copy-done.43) | copy-start | bytes 6148
  532.8 109.4 %copy-start.40 = (f32[256,2]{0,1:T(2,128)S(1)}, f32[256,2]{0,1:T(2,128)}, u32[]{:S(2)}) copy-start(f32[256,2]{0,1:T(2,128)} %copy-done.39) | copy-start | bytes 6148
  535.0 109.0 %copy-start.50 = (f32[512]{0:T(512)S(1)}, f32[512]{0:T(512)}, u32[]{:S(2)}) copy-start(f32[512]{0:T(512)} %get-tuple-element.70) | copy-start | bytes 6148
  535.0 109.0 %copy-start.51 = (f32[512]{0:T(512)S(1)}, f32[512]{0:T(512)}, u32[]{:S(2)}) copy-start(f32[512]{0:T(512)} %get-tuple-element.72) | copy-start | bytes 6148
  535.0 149.0 %copy-start.2 = (f32[256,2,512]{2,0,1:T(8,128)S(1)}, f32[256,2,512]{2,0,1:T(8,128)}, u32[]{:S(2)}) copy-start(f32[256,2,512]{2,0,1:T(8,128)} %get-tuple-element.83) | copy-start | bytes 3145732
  640.4 43.7 %copy-start.3 = (f32[256,2,512]{2,0,1:T(8,128)S(1)}, f32[256,2,512]{2,0,1:T(8,128)}, u32[]{:S(2)}) copy-start(f32[256,2,512]{2,0,1:T(8,128)} %reduce-scatter.14.cloned.1.call-done) | copy-start | bytes 3145732
  (9 other events, 8.7 us)
Sparse Core Ops, SparseCore 0:
  13.0 25.2 all-gather.4
  103.0 45.6 reduce-scatter.7
  151.7 22.5 all-gather.6
  234.9 44.5 reduce-scatter.9
  283.2 22.5 all-gather.8
  317.2 44.5 reduce-scatter.11
  368.5 22.5 all-gather.10
  515.4 78.2 all-reduce.4
  596.2 44.1 reduce-scatter.13
  644.2 64.2 reduce-scatter.17
  712.5 63.1 reduce-scatter.19
  779.4 60.9 reduce-scatter.15
